TPU v7x, 32 devices: a whole 2x2x4 slice. The times are simulated.
32 devices in a mesh: dp: 32 (over z, y, x, core).
Axes of the slice: x: 2, y: 2, z: 4, core: 2. Of those that a mesh axis runs over, the one named last changes fastest.
Arguments:
- features: bfloat16 [32, 32, 8, 2048], P('dp'), may hold values from -12 to 14, as said below
- slot_mask: int32 [32, 32, 8], P('dp'), may hold values from 0 to 1, as said below
- owner: int32 [32], replicated, may hold values from 0 to 31, each once
Outputs:
- class_mean: float32 [32, 2048], P('dp')
- class_cov: float32 [32, 2048, 2048], P('dp')
Inputs may be any that keep to these rules, and one draw needn't show every extreme that they name: `slot_mask`: every class has one device whose block of that class is full, so each class counts at least 8 images; about two thirds of slots hold images, with a fill rate that differs from class to class. The features of a class scatter around a class mean.
All inputs are finite; a program needn't handle non-finite values.
Results may differ from a plain program's by a relative error of at most 0.0003.
Values may be sent and summed in bfloat16 or wider, within the bound.
No kernel may reach another device: no remote copies, remote signals or barrier semaphores. Data moves between devices by JAX's collectives and lax.ppermute only.
A program may use at most 64 MiB of HBM per device.

v0:
```python
import jax
import jax.numpy as jnp
from jax import lax
from jax.sharding import PartitionSpec as P


def local(features, slot_mask, owner):
    devices = lax.axis_size("dp")
    blocks = features[0]
    weights = slot_mask[0]
    index = jnp.arange(devices, dtype=jnp.int32)
    match = (owner[None, :] == index[:, None]).astype(jnp.int32)
    class_of = jnp.sum(match * index[None, :], axis=1)
    ordered = jnp.take(blocks, class_of, axis=0)
    ordered_weights = jnp.take(weights, class_of, axis=0)
    arrived, arrived_weights = (
        lax.all_to_all(ordered, "dp", split_axis=0, concat_axis=0, tiled=True),
        lax.all_to_all(ordered_weights, "dp", split_axis=0, concat_axis=0, tiled=True),
    )
    width = arrived.shape[-1]
    rows = arrived.reshape(-1, width)
    slot_weight = arrived_weights.reshape(-1).astype(jnp.float32)
    count = jnp.sum(slot_weight)
    weight_row = slot_weight.astype(jnp.bfloat16)[None, :]
    mean = jnp.dot(weight_row, rows, preferred_element_type=jnp.float32)[0] / count
    weighted = rows * weight_row[0][:, None]
    second = lax.dot_general(
        weighted, rows, (((0,), (0,)), ((), ())), preferred_element_type=jnp.float32
    )
    cov = (second - count * mean[:, None] * mean[None, :]) / (count - 1.0)
    return (mean[None, :], cov[None, :, :])


def solution(mesh):
    return jax.shard_map(
        local,
        mesh=mesh,
        in_specs=(P("dp", None, None, None), P("dp", None, None), P()),
        out_specs=(P("dp", None), P("dp", None, None)),
        check_vma=False,
    )
```

profile of v0, /device:TPU:0, one launch (start us, length us, event | category | flops | bytes accessed | tf_op | source)
XLA Modules:
  0.0 55.6 jit_solution(9966688254646622913)
XLA Ops:
  0.6 0.0 copy-start
  0.6 0.9 %select_reduce_fusion = s32[32]{0:T(128)S(1)} fusion(s32[32]{0:T(128)} %param.5), kind=kLoop, calls=%fused_computation.9 | loop fusion | flops 3040 | bytes 256 | tf_op jit(solution)/shard_map/reduce_sum | solution.py:13
  1.5 0.8 %copy.18 = s32[1,32,8]{2,1,0:T(8,128)S(1)} copy(s32[1,32,8]{1,2,0:T(8,128)} %param.4) | data formatting | bytes 2048 | tf_op args[1]
  2.3 0.6 %gather_fusion = s32[32,8]{1,0:T(8,128)S(1)} fusion(s32[32,8]{1,0:T(8,128)S(1)} %bitcast.27, s32[1024]{0:T(1024)S(1)} %pad_clamp_fusion), kind=kCustom, calls=%fused_computation | custom fusion | bytes 2176 | tf_op jit(solution)/shard_map/jit(_take)/gather | solution.py:15
  2.9 0.7 %bitcast_select_fusion = s32[32,1,8]{2,0,1:T(8,128)} fusion(s32[32,8]{1,0:T(8,128)S(1)} %gather_fusion, pred[32]{0:T(512)(128)(4,1)S(1)} %compare_and_fusion), kind=kLoop, calls=%fused_computation.8 | loop fusion | flops 256 | bytes 2080 | tf_op jit(solution)/shard_map/jit(_take)/select_n | solution.py:15
  3.5 7.3 %all-to-all-start = ((s32[32,1,8]{2,1,0:T(1,128)}), s32[32,1,8]{2,1,0:T(1,128)S(1)}, u32[]{:S(2)}, u32[]{:S(2)}) async-start(s32[32,1,8]{2,1,0:T(1,128)} %bitcast.4), calls=%async_computation | async-start | bytes 32768 | tf_op jit(solution)/shard_map/all_to_all | solution.py:18
  10.9 0.0 copy-done
  10.9 0.6 %gather_fusion.1 = bf16[32,8,2048]{2,1,0:T(8,128)(2,1)S(1)} fusion(bf16[32,8,2048]{2,1,0:T(8,128)(2,1)S(1)} %bitcast.26, s32[1024]{0:T(1024)S(1)} %pad_clamp_fusion), kind=kCustom, calls=%fused_computation.1 | custom fusion | bytes 2097280 | tf_op jit(solution)/shard_map/jit(_take)/gather | solution.py:14
  11.5 1.1 %broadcast_select_fusion = bf16[32,8,2048]{2,1,0:T(8,128)(2,1)} fusion(bf16[32,8,2048]{2,1,0:T(8,128)(2,1)S(1)} %gather_fusion.1, pred[32]{0:T(512)(128)(4,1)S(1)} %compare_and_fusion), kind=kLoop, calls=%fused_computation.6 | loop fusion | flops 524288 | bytes 2097184 | tf_op jit(solution)/shard_map/jit(_take)/select_n | solution.py:14
  12.6 5.4 %all-to-all-done = s32[32,1,8]{2,1,0:T(1,128)S(1)} async-done(((s32[32,1,8]{2,1,0:T(1,128)}), s32[32,1,8]{2,1,0:T(1,128)S(1)}, u32[]{:S(2)}, u32[]{:S(2)}) %all-to-all-start) | async-done | bytes 1056 | tf_op jit(solution)/shard_map/all_to_all | solution.py:18
  18.1 2.6 %all-to-all-start.1 = ((bf16[32,8,2048]{2,1,0:T(8,128)(2,1)}), bf16[32,8,2048]{2,1,0:T(8,128)(2,1)S(1)}, u32[]{:S(2)}, u32[]{:S(2)}) async-start(bf16[32,8,2048]{2,1,0:T(8,128)(2,1)} %broadcast_select_fusion), calls=%async_computation.1 | async-start | bytes 2097152 | tf_op jit(solution)/shard_map/all_to_all | solution.py:17
  20.7 0.1 copy.20
  20.8 0.1 copy.21
  20.9 0.1 copy.22
  21.0 0.6 %convert_reduce_fusion = f32[]{:T(128)} fusion(s32[32,1,8]{0,2,1:T(8,128)S(1)} %copy.20), kind=kLoop, calls=%fused_computation.14 | loop fusion | flops 511 | bytes 1028 | tf_op jit(solution)/shard_map/reduce_sum | solution.py:23
  22.2 24.7 %all-to-all-done.1 = bf16[32,8,2048]{2,1,0:T(8,128)(2,1)S(1)} async-done(((bf16[32,8,2048]{2,1,0:T(8,128)(2,1)}), bf16[32,8,2048]{2,1,0:T(8,128)(2,1)S(1)}, u32[]{:S(2)}, u32[]{:S(2)}) %all-to-all-start.1) | async-done | bytes 1048608 | tf_op jit(solution)/shard_map/all_to_all | solution.py:17
  46.9 0.3 fusion.7
  47.2 0.7 %broadcast_multiply_fusion = (f32[2048]{0:T(1024)S(1)}, f32[2048]{0:T(1024)S(1)}) fusion(f32[]{:T(128)} %convert_reduce_fusion, f32[2048]{0:T(1024)S(1)} %bitcast.28), kind=kLoop, calls=%fused_computation.12 | loop fusion | flops 4096 | bytes 24580 | tf_op jit(solution)/shard_map/mul | solution.py:30
  47.9 0.0 copy-start.1
  47.9 7.6 %fusion.1 = f32[1,2048,2048]{2,1,0:T(8,128)} fusion(bf16[32,8,2048]{2,1,0:T(8,128)(2,1)S(1)} %all-to-all-done.1, f32[]{:T(128)S(6)} %sub.7, f32[2048]{0:T(1024)S(1)} %get-tuple-element.3, f32[2048]{0:T(1024)S(1)} %get-tuple-element.2, bf16[32,8]{1,0:T(8,128)(2,1)S(1)} %copy.21), kind=kOutput, calls=%fused_computation.4 | convolution fusion | flops 2160590848 | bytes 17842692 | tf_op jit(solution)/shard_map/dot_general | solution.py:27
  55.5 0.0 copy-done.1
  (4 shorter events, 0.0 us)
Async XLA Ops:
  0.6 10.3 %copy-start = (bf16[1,32,8,2048]{3,2,1,0:T(8,128)(2,1)S(1)}, bf16[1,32,8,2048]{3,2,1,0:T(8,128)(2,1)}, u32[]{:S(2)}) copy-start(bf16[1,32,8,2048]{3,2,1,0:T(8,128)(2,1)} %param.3) | copy-start | bytes 3145732
  3.5 14.5 %all-to-all-start = ((s32[32,1,8]{2,1,0:T(1,128)}), s32[32,1,8]{2,1,0:T(1,128)S(1)}, u32[]{:S(2)}, u32[]{:S(2)}) async-start(s32[32,1,8]{2,1,0:T(1,128)} %bitcast.4), calls=%async_computation | async-start | bytes 32768 | tf_op jit(solution)/shard_map/all_to_all | solution.py:18
  18.1 28.8 %all-to-all-start.1 = ((bf16[32,8,2048]{2,1,0:T(8,128)(2,1)}), bf16[32,8,2048]{2,1,0:T(8,128)(2,1)S(1)}, u32[]{:S(2)}, u32[]{:S(2)}) async-start(bf16[32,8,2048]{2,1,0:T(8,128)(2,1)} %broadcast_select_fusion), calls=%async_computation.1 | async-start | bytes 2097152 | tf_op jit(solution)/shard_map/all_to_all | solution.py:17
  47.9 7.6 %copy-start.1 = (f32[2048]{0:T(1024)}, f32[2048]{0:T(1024)S(1)}, u32[]{:S(2)}) copy-start(f32[2048]{0:T(1024)S(1)} %get-tuple-element.3) | copy-start | bytes 24580
where the time goes:
time: 55.8 us; the launch traced here: 55.6 us
  waiting for transfers between devices  30.1 us (54%)
  starting transfers between devices  9.97 us (18%)
  matrix products  7.97 us (14%)
  other arithmetic  3.95 us (7%)
  local copies, waits for them, and re-layouts  2.22 us (4%)
  between operations  1.36 us (2%)
    all_to_all x1, waiting for transfers between devices, local(): lax.all_to_all(ordered, 'dp', split_axis=0, concat_axis=0, tiled=True)  24.7 us
    dot_general x1, matrix products, local(): lax.dot_general(weighted, rows, (((0,), (0,)), ((), ())), preferred_eleme...  7.63 us
    all_to_all x1, starting transfers between devices, local(): lax.all_to_all(ordered_weights, 'dp', split_axis=0, concat_axis=0, tiled=...  7.33 us
    all_to_all x1, waiting for transfers between devices, local(): lax.all_to_all(ordered_weights, 'dp', split_axis=0, concat_axis=0, tiled=...  5.41 us
    all_to_all x1, starting transfers between devices, local(): lax.all_to_all(ordered, 'dp', split_axis=0, concat_axis=0, tiled=True)  2.65 us
    select_n x1, other arithmetic, local(): ordered = jnp.take(blocks, class_of, axis=0)  1.13 us
  transfers between devices with their start and end apart: 2, of which 2 were waited for; matrix products, arithmetic and copies ran while one was open for 5% of the time, Pallas kernels for 0%

commit v1 on v0

v1 whole, which is shorter than its diff:
```python
import functools

import jax
import jax.numpy as jnp
from jax import lax
from jax.experimental import pallas as pl
from jax.experimental.pallas import tpu as pltpu
from jax.sharding import PartitionSpec as P

LANES = 128
MARK = 2.0**100
LIMIT = 2.0**90


def pack_kernel(owner_ref, mask_ref, blocks_ref, out_ref):
    classes, slots, width = blocks_ref.shape
    mask = mask_ref[...].astype(jnp.float32)
    lane = lax.broadcasted_iota(jnp.int32, mask.shape, 1)

    def one(c, carry):
        weight = jnp.sum(jnp.where(lane == c, mask, 0.0), axis=1, keepdims=True)
        place = owner_ref[c]
        wide = jnp.broadcast_to(weight, (slots, LANES)).astype(jnp.bfloat16)
        mark = ((1.0 - weight) * MARK).astype(jnp.bfloat16)
        for j in range(0, width, LANES):
            tile = blocks_ref[c, :, j : j + LANES] * wide
            if j == 0:
                tile = tile + jnp.broadcast_to(mark, (slots, LANES))
            out_ref[place, :, j : j + LANES] = tile
        return carry

    lax.fori_loop(0, classes, one, 0, unroll=4)


def cov_kernel(rows_ref, mean_ref, cov_ref, clean, ones, shift, scal):
    step = pl.program_id(0)
    height = cov_ref.shape[1]

    @pl.when(step == 0)
    def _():
        first = rows_ref[:, :LANES]
        held = first.astype(jnp.float32) < LIMIT
        clean[:, :LANES] = jnp.where(held, first.astype(jnp.float32), 0.0).astype(jnp.bfloat16)
        clean[:, LANES:] = rows_ref[:, LANES:]
        weight = held.astype(jnp.float32)
        ones[...] = weight.astype(jnp.bfloat16)
        count = jnp.sum(weight, axis=0, keepdims=True)[:, :1]
        total = jnp.sum(clean[...].astype(jnp.float32), axis=0, keepdims=True)
        mean = total / count
        mean_ref[...] = mean
        shift[...] = mean / (count - 1.0)
        scal[...] = jnp.broadcast_to(1.0 / (count - 1.0), scal.shape)

    at = pl.ds(pl.multiple_of(step * height, height), height)
    left = clean[:, at]
    contract = (((0,), (0,)), ((), ()))
    second = lax.dot_general(left, clean[...], contract, preferred_element_type=jnp.float32)
    total = lax.dot_general(left, ones[...], contract, preferred_element_type=jnp.float32)[:, :1]
    cov_ref[0] = second * scal[:, :1] - total * shift[...]


def local(features, slot_mask, owner):
    blocks = features[0]
    classes, slots, width = blocks.shape
    mask = jnp.swapaxes(slot_mask[0], 0, 1)
    vmem = pl.BlockSpec(memory_space=pltpu.VMEM)
    packed = pl.pallas_call(
        pack_kernel,
        out_shape=jax.ShapeDtypeStruct(blocks.shape, blocks.dtype),
        in_specs=[pl.BlockSpec(memory_space=pltpu.SMEM), vmem, vmem],
        out_specs=vmem,
        name="pack",
    )(owner, mask, blocks)
    arrived = lax.all_to_all(packed, "dp", split_axis=0, concat_axis=0, tiled=True)
    rows = arrived.reshape(-1, width)
    depth = rows.shape[0]
    height = 128
    mean, cov = pl.pallas_call(
        cov_kernel,
        grid=(width // height,),
        out_shape=(
            jax.ShapeDtypeStruct((1, width), jnp.float32),
            jax.ShapeDtypeStruct((1, width, width), jnp.float32),
        ),
        in_specs=[pl.BlockSpec((depth, width), lambda i: (0, 0))],
        out_specs=(
            pl.BlockSpec((1, width), lambda i: (0, 0)),
            pl.BlockSpec((1, height, width), lambda i: (0, i, 0)),
        ),
        scratch_shapes=[
            pltpu.VMEM((depth, width), jnp.bfloat16),
            pltpu.VMEM((depth, LANES), jnp.bfloat16),
            pltpu.VMEM((1, width), jnp.float32),
            pltpu.VMEM((1, LANES), jnp.float32),
        ],
        name="covariance",
    )(rows)
    return mean, cov


def solution(mesh):
    return jax.shard_map(
        local,
        mesh=mesh,
        in_specs=(P("dp", None, None, None), P("dp", None, None), P()),
        out_specs=(P("dp", None), P("dp", None, None)),
        check_vma=False,
    )
```

time: 55.8 us -> 51.4 us (0.921)
  blocking collectives: 0 us -> 33.6 us
  waiting for transfers between devices: 30.1 us -> 0 us
  Pallas kernels: 0 us -> 16.8 us
  starting transfers between devices: 9.97 us -> 0 us
  matrix products: 7.97 us -> 0 us
  other arithmetic: 3.95 us -> 0 us
  local copies, waits for them, and re-layouts: 2.22 us -> 0 us
  between operations: 1.36 us -> 0.63 us
    all_to_all x0 -> x1, blocking collectives: none -> 33.6 us  [local(): lax.all_to_all(packed, 'dp', split_axis=0, concat_axis=0, tiled=True)]
    all_to_all x2 -> x0, waiting for transfers between devices: 30.1 us -> none  [the longest x1 24.7 us: local(): lax.all_to_all(ordered, 'dp', split_axis=0, concat_axis=0, tiled=True)]
    pallas_call x0 -> x2, Pallas kernels: none -> 16.8 us  [the longest x1 13.9 us: local(): pl.pallas_call(cov_kernel, grid=(width // height,), out_shape=(jax.ShapeD...]
    all_to_all x2 -> x0, starting transfers between devices: 9.97 us -> none  [the longest x1 7.33 us: local(): lax.all_to_all(ordered_weights, 'dp', split_axis=0, concat_axis=0, tiled=...]
    dot_general x2 -> x0, matrix products: 7.97 us -> none  [the longest x1 7.63 us: local(): lax.dot_general(weighted, rows, (((0,), (0,)), ((), ())), preferred_eleme...]
    select_n x3 -> x0, other arithmetic: 1.81 us -> none  [the longest x1 1.13 us: local(): ordered = jnp.take(blocks, class_of, axis=0)]
    reduce_sum x2 -> x0, other arithmetic: 1.46 us -> none  [the longest x1 0.85 us: local(): class_of = jnp.sum(match * index[None, :], axis=1)]
    gather x2 -> x0, local copies, waits for them, and re-layouts: 1.19 us -> none  [the longest x1 0.61 us: local(): ordered = jnp.take(blocks, class_of, axis=0)]
  transfers between devices with their start and end apart: 2 -> 0, of which waited for: 2 -> 0; matrix products, arithmetic and copies ran while one was open for 5% -> 0% of each run, Pallas kernels for 0% -> 0%
where the time goes in v1:
time: 51.4 us; the launch traced here: 51.1 us
  blocking collectives  33.6 us (65%)
  Pallas kernels  16.8 us (33%)
  between operations  0.63 us (1%)
    all_to_all x1, blocking collectives, local(): lax.all_to_all(packed, 'dp', split_axis=0, concat_axis=0, tiled=True)  33.6 us
    pallas_call x1, Pallas kernels, local(): pl.pallas_call(cov_kernel, grid=(width // height,), out_shape=(jax.ShapeD...  13.9 us
    pallas_call x1, Pallas kernels, local(): pl.pallas_call(pack_kernel, out_shape=jax.ShapeDtypeStruct(blocks.shape,...  2.98 us

profile of v1, /device:TPU:0, one launch (start us, length us, event | category | flops | bytes accessed | tf_op | source)
XLA Modules:
  0.0 51.1 jit_solution(11651816966138271727)
XLA Ops:
  0.6 3.0 %pack.1 = bf16[32,8,2048]{2,1,0:T(8,128)(2,1)} custom-call(s32[32]{0:T(128)} %owner_ref.1, s32[8,32]{1,0:T(8,128)} %bitcast.7, bf16[32,8,2048]{2,1,0:T(8,128)(2,1)} %bitcast.6), custom_call_target="tpu_custom_call" | custom-call | tf_op jit(solution)/shard_map/pack/pallas_call | solution.py:67
  3.6 33.6 %all_to_all.5 = bf16[32,8,2048]{2,1,0:T(8,128)(2,1)} all-to-all(bf16[32,8,2048]{2,1,0:T(8,128)(2,1)} %pack.1), channel_id=1, replica_groups=mesh['dp'=32] {'dp'}, dimensions={0} | all-to-all | bytes 2097152 | tf_op jit(solution)/shard_map/all_to_all | solution.py:74
  37.3 13.9 %covariance.1 = (f32[1,2048]{1,0:T(1,128)}, f32[1,2048,2048]{2,1,0:T(8,128)}) custom-call(bf16[256,2048]{1,0:T(8,128)(2,1)} %bitcast.5), custom_call_target="tpu_custom_call" | custom-call | tf_op jit(solution)/shard_map/covariance/pallas_call | solution.py:78

commit v2 on v1

v2 whole, which is shorter than its diff:
```python
import jax
import jax.numpy as jnp
from jax import lax
from jax.experimental import pallas as pl
from jax.experimental.pallas import tpu as pltpu
from jax.sharding import PartitionSpec as P

LANES = 128
MARK = 2.0**100
LIMIT = 2.0**90
MIB = 2**20


def pack_kernel(groups, owner_hbm, mask_hbm, blocks_hbm, out_ref, owner, mask, blocks, wide, small, big):
    classes, slots, width = out_ref.shape
    each = classes // groups
    to_owner = pltpu.make_async_copy(owner_hbm, owner, small.at[0])
    to_mask = pltpu.make_async_copy(mask_hbm, mask, small.at[1])
    to_mask.start()
    to_owner.start()
    loads = []
    for g in range(groups):
        part = pl.ds(g * each, each)
        loads.append(pltpu.make_async_copy(blocks_hbm.at[part], blocks.at[part], big.at[g]))
        loads[-1].start()
    to_mask.wait()
    for c in range(classes):
        weight = mask[:, c : c + 1].astype(jnp.float32)
        wide[c] = jnp.broadcast_to(weight, (slots, LANES)).astype(jnp.bfloat16)
    to_owner.wait()
    for g in range(groups):
        loads[g].wait()

        def one(i, carry):
            c = g * each + i
            place = owner[c]
            weight = wide[c]
            for j in range(0, width, LANES):
                tile = blocks[c, :, j : j + LANES] * weight
                if j == 0:
                    tile = tile + (1.0 - weight) * MARK
                out_ref[place, :, j : j + LANES] = tile
            return carry

        lax.fori_loop(0, each, one, 0, unroll=min(4, each))


def cov_kernel(rows_ref, mean_ref, cov_ref, clean, ones, shift, scale, mean, left, out, mean_sem, cov_sem):
    depth, width = clean.shape
    first = rows_ref[:, :LANES].astype(jnp.float32)
    held = first < LIMIT
    clean[:, :LANES] = jnp.where(held, first, 0.0).astype(jnp.bfloat16)
    clean[:, LANES:] = rows_ref[:, LANES:]
    weight = held.astype(jnp.float32)
    ones[...] = weight.astype(jnp.bfloat16)
    count = jnp.sum(weight, axis=0, keepdims=True)
    scale[...] = 1.0 / (count - 1.0)
    for j in range(0, width, LANES):
        part = slice(j, j + LANES)
        total = jnp.sum(clean[:, part].astype(jnp.float32), axis=0, keepdims=True)
        mean[:, part] = total / count
        shift[:, part] = total / count * scale[...]
    mean_copy = pltpu.make_async_copy(mean, mean_ref, mean_sem)
    mean_copy.start()

    contract = (((1,), (0,)), ((), ()))
    tile = 2 * LANES

    def block(at, height):
        left[:height] = clean[:, pl.ds(at, height)].T
        total = lax.dot_general(left[:height], ones[...], contract, preferred_element_type=jnp.float32)
        for j in range(0, width, tile):
            second = lax.dot_general(
                left[:height], clean[:, j : j + tile], contract, preferred_element_type=jnp.float32
            )
            for k in range(0, tile, LANES):
                part = slice(j + k, j + k + LANES)
                out[pl.ds(at, height), part] = second[:, k : k + LANES] * scale[...] - total * shift[:, part]
        here = pl.ds(at, height)
        pltpu.make_async_copy(out.at[here], cov_ref.at[0, here], cov_sem).start()

    block(0, LANES)
    block(LANES, LANES)

    def step(i, carry):
        block(pl.multiple_of(i * tile, tile), tile)
        return carry

    lax.fori_loop(1, width // tile, step, 0)
    pltpu.make_async_copy(out, cov_ref.at[0], cov_sem).wait()
    mean_copy.wait()


def local(features, slot_mask, owner):
    blocks = features[0]
    classes, slots, width = blocks.shape
    mask = jnp.swapaxes(slot_mask[0], 0, 1)
    vmem = pl.BlockSpec(memory_space=pltpu.VMEM)
    hbm = pl.BlockSpec(memory_space=pltpu.HBM)
    groups = 4
    packed = pl.pallas_call(
        lambda *refs: pack_kernel(groups, *refs),
        out_shape=jax.ShapeDtypeStruct(blocks.shape, blocks.dtype),
        in_specs=[hbm, hbm, hbm],
        out_specs=vmem,
        scratch_shapes=[
            pltpu.SMEM((classes,), jnp.int32),
            pltpu.VMEM((slots, classes), jnp.int32),
            pltpu.VMEM(blocks.shape, blocks.dtype),
            pltpu.VMEM((classes, slots, LANES), blocks.dtype),
            pltpu.SemaphoreType.DMA((2,)),
            pltpu.SemaphoreType.DMA((groups,)),
        ],
        compiler_params=pltpu.CompilerParams(vmem_limit_bytes=16 * MIB),
        name="pack",
    )(*(pltpu.with_memory_space_constraint(a, pltpu.HBM) for a in (owner, mask, blocks)))
    arrived = lax.all_to_all(packed, "dp", split_axis=0, concat_axis=0, tiled=True)
    rows = arrived.reshape(-1, width)
    depth = rows.shape[0]
    mean, cov = pl.pallas_call(
        cov_kernel,
        out_shape=(
            jax.ShapeDtypeStruct((1, width), jnp.float32),
            jax.ShapeDtypeStruct((1, width, width), jnp.float32),
        ),
        in_specs=[vmem],
        out_specs=(hbm, hbm),
        scratch_shapes=[
            pltpu.VMEM((depth, width), jnp.bfloat16),
            pltpu.VMEM((depth, LANES), jnp.bfloat16),
            pltpu.VMEM((1, width), jnp.float32),
            pltpu.VMEM((1, LANES), jnp.float32),
            pltpu.VMEM((1, width), jnp.float32),
            pltpu.VMEM((2 * LANES, depth), jnp.bfloat16),
            pltpu.VMEM((width, width), jnp.float32),
            pltpu.SemaphoreType.DMA,
            pltpu.SemaphoreType.DMA,
        ],
        compiler_params=pltpu.CompilerParams(vmem_limit_bytes=40 * MIB),
        name="covariance",
    )(rows)
    return mean, cov


def solution(mesh):
    return jax.shard_map(
        local,
        mesh=mesh,
        in_specs=(P("dp", None, None, None), P("dp", None, None), P()),
        out_specs=(P("dp", None), P("dp", None, None)),
        check_vma=False,
    )
```

time: 51.4 us -> 42.1 us (0.82)
  Pallas kernels: 16.8 us -> 7.96 us
    pallas_call x2, Pallas kernels: 16.8 us -> 7.96 us  [the longest x1 6.63 us: local(): pl.pallas_call(cov_kernel, out_shape=(jax.ShapeDtypeStruct((1, width), jn...]
where the time goes in v2:
time: 42.1 us; the launch traced here: 41.9 us
  blocking collectives  33.3 us (79%)
  Pallas kernels  7.96 us (19%)
  between operations  0.64 us (2%)
    all_to_all x1, blocking collectives, local(): lax.all_to_all(packed, 'dp', split_axis=0, concat_axis=0, tiled=True)  33.3 us
    pallas_call x1, Pallas kernels, local(): pl.pallas_call(cov_kernel, out_shape=(jax.ShapeDtypeStruct((1, width), jn...  6.63 us
    pallas_call x1, Pallas kernels, local(): pl.pallas_call(lambda *refs: pack_kernel(groups, *refs), out_shape=jax.Sh...  1.32 us

profile of v2, /device:TPU:0, one launch (start us, length us, event | category | flops | bytes accessed | tf_op | source)
XLA Modules:
  0.0 41.9 jit_solution(16115067648289130198)
XLA Ops:
  0.6 1.3 %pack.1 = bf16[32,8,2048]{2,1,0:T(8,128)(2,1)S(1)} custom-call(s32[32]{0:T(128)} %refs_0_.1, s32[8,32]{1,0:T(8,128)} %bitcast.7, bf16[32,8,2048]{2,1,0:T(8,128)(2,1)} %bitcast.6), custom_call_target="tpu_custom_call" | custom-call | tf_op jit(solution)/shard_map/pack/pallas_call | solution.py:101
  2.0 33.3 %all_to_all.5 = bf16[32,8,2048]{2,1,0:T(8,128)(2,1)S(1)} all-to-all(bf16[32,8,2048]{2,1,0:T(8,128)(2,1)S(1)} %pack.1), channel_id=1, replica_groups=mesh['dp'=32] {'dp'}, dimensions={0} | all-to-all | bytes 2097152 | tf_op jit(solution)/shard_map/all_to_all | solution.py:117
  35.3 6.6 %covariance.1 = (f32[1,2048]{1,0:T(1,128)}, f32[1,2048,2048]{2,1,0:T(8,128)}) custom-call(bf16[256,2048]{1,0:T(8,128)(2,1)S(1)} %bitcast.5), custom_call_target="tpu_custom_call" | custom-call | tf_op jit(solution)/shard_map/covariance/pallas_call | solution.py:120

commit v3 on v2

v3 whole, which is shorter than its diff:
```python
import jax
import jax.numpy as jnp
from jax import lax
from jax.experimental import pallas as pl
from jax.experimental.pallas import tpu as pltpu
from jax.sharding import PartitionSpec as P


AXIS = "dp"
LANES = 128
TILE = 2 * LANES
MARK = 2.0**100
LIMIT = 2.0**90
MIB = 2**20

VMEM = pl.BlockSpec(memory_space=pltpu.VMEM)
HBM = pl.BlockSpec(memory_space=pltpu.HBM)


def factors(devices):
    bits = devices.bit_length() - 1
    assert devices == 1 << bits
    inner = 1 << (bits + 1) // 2
    return devices // inner, inner


def late_width(width):
    return width * 6 // 16 // LANES * LANES


def tiles(width):
    return [(at, min(TILE, width - at)) for at in range(0, width, TILE)]


def pack_kernel(groups, inner, lead, owner_hbm, mask_hbm, blocks_hbm, early_hbm, late_ref, lead_ref, owner, mask, blocks, wide, small, big, out_sem):
    classes, slots, width = blocks.shape
    early = early_hbm.shape[-1]
    each = classes // groups
    to_owner = pltpu.make_async_copy(owner_hbm, owner, small.at[0])
    to_mask = pltpu.make_async_copy(mask_hbm, mask, small.at[1])
    to_mask.start()
    to_owner.start()
    loads = []
    for g in range(groups):
        part = pl.ds(g * each, each)
        loads.append(pltpu.make_async_copy(blocks_hbm.at[part], blocks.at[part], big.at[g]))
        loads[-1].start()
    me = lax.axis_index(AXIS)
    to_mask.wait()
    for c in range(classes):
        weight = mask[:, c : c + 1].astype(jnp.float32)
        wide[c] = jnp.broadcast_to(weight, (slots, LANES)).astype(jnp.bfloat16)
    to_owner.wait()
    for g in range(groups):
        loads[g].wait()

        def one(i, carry):
            c = g * each + i
            weight = wide[c]
            for j in range(0, early, LANES):
                tile = blocks[c, :, j : j + LANES] * weight
                if j == 0:
                    tile = tile + (1.0 - weight) * MARK
                blocks[c, :, j : j + LANES] = tile
            return carry

        lax.fori_loop(0, each, one, 0, unroll=min(4, each))

        def send(i, carry):
            c = g * each + i
            pltpu.make_async_copy(blocks.at[c, :, pl.ds(0, early)], early_hbm.at[owner[c]], out_sem).start()
            return carry

        lax.fori_loop(0, each, send, 0, unroll=min(4, each))

    def sort(c, carry):
        flip = jnp.bitwise_xor(owner[c], me)
        d = flip // inner
        q = flip % inner
        weight = wide[c]
        for j in range(early, width, LANES):
            late_ref[q, d, :, j - early : j - early + LANES] = blocks[c, :, j : j + LANES] * weight

        @pl.when(d == lead)
        def _():
            lead_ref[q] = late_ref[q, d]

        return carry

    lax.fori_loop(0, classes, sort, 0, unroll=4)
    pltpu.make_async_copy(blocks.at[:, :, pl.ds(0, early)], early_hbm, out_sem).wait()


def mix_kernel(lead, late_ref, lead_ref, *outs):
    for q, out in enumerate(outs):
        for d in range(out.shape[0]):
            out[d] = lead_ref[q] if d == lead else late_ref[q, d]


def repack_kernel(inner, *refs):
    held, sends = refs[:inner], refs[inner:]
    for d, send in enumerate(sends):
        for q in range(inner):
            send[q] = held[q][d]


def dot(left, right):
    return lax.dot_general(left, right, (((1,), (0,)), ((), ())), preferred_element_type=jnp.float32)


def means_of(rows, each, mean, shift, scale, at=0):
    for j in range(0, rows.shape[1], LANES):
        part = slice(j, j + LANES)
        value = jnp.sum(rows[:, part].astype(jnp.float32), axis=0, keepdims=True) * each
        mean[:, at + j : at + j + LANES] = value
        shift[:, part] = value * scale


def early_kernel(rows_ref, mean_ref, cov_ref, clean, turned, ones, stats, shift, out, cov_sem):
    width = rows_ref.shape[1]
    first = rows_ref[:, :LANES].astype(jnp.float32)
    held = first < LIMIT
    weight = held.astype(jnp.float32)
    ones[...] = weight.astype(jnp.bfloat16)
    count = jnp.sum(weight, axis=0, keepdims=True)
    each = 1.0 / count
    scale = 1.0 / (count - 1.0)
    stats[0:1] = each
    stats[1:2] = scale
    clean[:, :LANES] = jnp.where(held, first, 0.0).astype(jnp.bfloat16)
    clean[:, LANES:] = rows_ref[:, LANES:]
    means_of(clean, each, mean_ref, shift, scale)

    def block(at, height):
        here = pl.ds(at, height)
        turned[here] = clean[:, here].T
        total = dot(turned[here], ones[...])
        for j, wide in tiles(width):
            second = dot(turned[here], clean[:, j : j + wide])
            for k in range(0, wide, LANES):
                part = slice(j + k, j + k + LANES)
                out[here, part] = second[:, k : k + LANES] * scale - total * shift[:, part]
        pltpu.make_async_copy(out.at[here], cov_ref.at[0, here, pl.ds(0, width)], cov_sem).start()

    def step(i, carry):
        block(pl.multiple_of(i * TILE, TILE), TILE)
        return carry

    lax.fori_loop(0, width // TILE, step, 0)
    if width % TILE:
        block(width // TILE * TILE, width % TILE)
    pltpu.make_async_copy(out, cov_ref.at[0, pl.ds(0, width), pl.ds(0, width)], cov_sem).wait()


def late_kernel(inner, pieces, *refs):
    clean, turned, ones, stats, early_mean = refs[:5]
    parts = refs[5 : 5 + pieces]
    _, mean_ref, cov_ref, gathered, tail, mean, shift, early_shift, left, right, low, mean_sem, cov_sem = refs[5 + pieces :]
    depth, early = clean.shape
    late = tail.shape[-1]
    me = lax.axis_index(AXIS)
    for d in range(pieces):
        for q in range(inner):
            gathered[jnp.bitwise_xor(me, d * inner + q)] = parts[d][q]
    tail[...] = gathered[...].reshape(depth, late)
    each = stats[0:1]
    scale = stats[1:2]
    means_of(tail, each, mean, shift, scale, early)

    def beside(at, height):
        here = pl.ds(at, height)
        total = dot(turned[here], ones[...])
        for j, wide in tiles(late):
            second = dot(turned[here], tail[:, j : j + wide])
            for k in range(0, wide, LANES):
                part = slice(j + k, j + k + LANES)
                right[here, part] = second[:, k : k + LANES] * scale - total * shift[:, part]
        pltpu.make_async_copy(right.at[here], cov_ref.at[0, here, pl.ds(early, late)], cov_sem).start()

    for at, height in tiles(early):
        beside(at, height)

    mean[:, :early] = early_mean[...]
    mean_copy = pltpu.make_async_copy(mean, mean_ref, mean_sem)
    mean_copy.start()
    for j in range(0, early, LANES):
        early_shift[:, j : j + LANES] = early_mean[:, j : j + LANES] * scale

    def below(at, height):
        here = pl.ds(at, height)
        left[:height] = tail[:, here].T
        total = dot(left[:height], ones[...])
        for source, sums, base, span in ((clean, early_shift, 0, early), (tail, shift, early, late)):
            for j, wide in tiles(span):
                second = dot(left[:height], source[:, j : j + wide])
                for k in range(0, wide, LANES):
                    part = slice(j + k, j + k + LANES)
                    value = second[:, k : k + LANES] * scale - total * sums[:, part]
                    low[here, base + j + k : base + j + k + LANES] = value
        pltpu.make_async_copy(low.at[here], cov_ref.at[0, pl.ds(early + at, height)], cov_sem).start()

    for at, height in tiles(late):
        below(at, height)
    pltpu.make_async_copy(right, cov_ref.at[0, pl.ds(0, early), pl.ds(early, late)], cov_sem).wait()
    pltpu.make_async_copy(low, cov_ref.at[0, pl.ds(early, late)], cov_sem).wait()
    mean_copy.wait()


def local(features, slot_mask, owner):
    devices = lax.axis_size(AXIS)
    outer, inner = factors(devices)
    blocks = features[0]
    classes, slots, width = blocks.shape
    late = late_width(width)
    early = width - late
    depth = devices * slots
    bf16, f32 = jnp.bfloat16, jnp.float32
    mask = jnp.swapaxes(slot_mask[0], 0, 1)
    groups = 8

    inputs = [pltpu.with_memory_space_constraint(a, pltpu.HBM) for a in (owner, mask, blocks)]

    lead = outer // 2
    packed, sorted_late, leading = pl.pallas_call(
        lambda *refs: pack_kernel(groups, inner, lead, *refs),
        out_shape=(
            jax.ShapeDtypeStruct((devices, slots, early), bf16),
            jax.ShapeDtypeStruct((inner, outer, slots, late), bf16),
            jax.ShapeDtypeStruct((inner, slots, late), bf16),
        ),
        in_specs=[HBM, HBM, HBM],
        out_specs=(HBM, VMEM, VMEM),
        scratch_shapes=[
            pltpu.SMEM((classes,), jnp.int32),
            pltpu.VMEM((slots, classes), jnp.int32),
            pltpu.VMEM(blocks.shape, bf16),
            pltpu.VMEM((classes, slots, LANES), bf16),
            pltpu.SemaphoreType.DMA((2,)),
            pltpu.SemaphoreType.DMA((groups,)),
            pltpu.SemaphoreType.DMA,
        ],
        compiler_params=pltpu.CompilerParams(vmem_limit_bytes=16 * MIB),
        name="pack",
    )(*inputs)

    def far(d, value):
        return lax.ppermute(value, AXIS, [(i, i ^ (d * inner)) for i in range(devices)])

    led = far(lead, leading)
    arrived = lax.all_to_all(packed, AXIS, split_axis=0, concat_axis=0, tiled=True)
    mixed = pl.pallas_call(
        lambda *refs: mix_kernel(lead, *refs),
        out_shape=(jax.ShapeDtypeStruct((outer, slots, late), bf16),) * inner,
        in_specs=[VMEM] * 2,
        out_specs=(VMEM,) * inner,
        compiler_params=pltpu.CompilerParams(vmem_limit_bytes=16 * MIB),
        name="mix",
    )(sorted_late, led)
    held = [mixed[0]]
    for q in range(1, inner):
        held.append(lax.ppermute(mixed[q], AXIS, [(i, i ^ q) for i in range(devices)]))
    parts = pl.pallas_call(
        lambda *refs: repack_kernel(inner, *refs),
        out_shape=(jax.ShapeDtypeStruct((inner, slots, late), bf16),) * outer,
        in_specs=[VMEM] * inner,
        out_specs=(VMEM,) * outer,
        compiler_params=pltpu.CompilerParams(vmem_limit_bytes=16 * MIB),
        name="repack",
    )(*held)
    parts = [part if d in (0, lead) else far(d, part) for d, part in enumerate(parts)]
    rows = arrived.reshape(depth, early)
    early_mean, begun, *prepared = pl.pallas_call(
        early_kernel,
        out_shape=(
            jax.ShapeDtypeStruct((1, early), f32),
            jax.ShapeDtypeStruct((1, width, width), f32),
            jax.ShapeDtypeStruct((depth, early), bf16),
            jax.ShapeDtypeStruct((early, depth), bf16),
            jax.ShapeDtypeStruct((depth, LANES), bf16),
            jax.ShapeDtypeStruct((8, LANES), f32),
        ),
        in_specs=[VMEM],
        out_specs=(VMEM, HBM, VMEM, VMEM, VMEM, VMEM),
        scratch_shapes=[
            pltpu.VMEM((1, early), f32),
            pltpu.VMEM((early, early), f32),
            pltpu.SemaphoreType.DMA,
        ],
        compiler_params=pltpu.CompilerParams(vmem_limit_bytes=40 * MIB),
        cost_estimate=pl.CostEstimate(
            flops=2 * depth * early * early, bytes_accessed=4 * early * early, transcendentals=0
        ),
        name="early_covariance",
    )(rows)
    mean, cov = pl.pallas_call(
        lambda *refs: late_kernel(inner, outer, *refs),
        out_shape=(
            jax.ShapeDtypeStruct((1, width), f32),
            jax.ShapeDtypeStruct((1, width, width), f32),
        ),
        in_specs=[VMEM] * (5 + outer) + [HBM],
        out_specs=(HBM, HBM),
        scratch_shapes=[
            pltpu.VMEM((devices, slots, late), bf16),
            pltpu.VMEM((depth, late), bf16),
            pltpu.VMEM((1, width), f32),
            pltpu.VMEM((1, late), f32),
            pltpu.VMEM((1, early), f32),
            pltpu.VMEM((TILE, depth), bf16),
            pltpu.VMEM((early, late), f32),
            pltpu.VMEM((late, width), f32),
            pltpu.SemaphoreType.DMA,
            pltpu.SemaphoreType.DMA,
        ],
        input_output_aliases={5 + outer: 1},
        compiler_params=pltpu.CompilerParams(vmem_limit_bytes=40 * MIB),
        cost_estimate=pl.CostEstimate(
            flops=2 * depth * (width * width - early * early),
            bytes_accessed=4 * (width * width - early * early),
            transcendentals=0,
        ),
        name="late_covariance",
    )(*prepared, early_mean, *parts, begun)
    return mean, cov


def solution(mesh):
    return jax.shard_map(
        local,
        mesh=mesh,
        in_specs=(P(AXIS, None, None, None), P(AXIS, None, None), P()),
        out_specs=(P(AXIS, None), P(AXIS, None, None)),
        check_vma=False,
    )
```

time: 42.1 us -> 54.3 us (1.29)
  blocking collectives: 33.3 us -> 0 us
  waiting for transfers between devices: 0 us -> 25.6 us
  starting transfers between devices: 0 us -> 17.9 us
  Pallas kernels: 7.96 us -> 9.85 us
    all_to_all x1 -> x0, blocking collectives: 33.3 us -> none  [local(): lax.all_to_all(packed, 'dp', split_axis=0, concat_axis=0, tiled=True)]
    ppermute x0 -> x10, waiting for transfers between devices: none -> 25.6 us  [the longest x3 21.3 us: far(): lax.ppermute(value, AXIS, [(i, i ^ d * inner) for i in range(devices)])]
    ppermute x0 -> x10, starting transfers between devices: none -> 10.6 us  [the longest x7 6.31 us: local(): lax.ppermute(mixed[q], AXIS, [(i, i ^ q) for i in range(devices)])]
    all_to_all x0 -> x1, starting transfers between devices: none -> 7.33 us  [local(): lax.all_to_all(packed, AXIS, split_axis=0, concat_axis=0, tiled=True)]
    pallas_call x2 -> x5, Pallas kernels: 7.96 us -> 9.85 us  [the longest x1 4.35 us: local(): pl.pallas_call(lambda *refs: late_kernel(inner, outer, *refs), out_shape=...]
  transfers between devices with their start and end apart: 0 -> 11, of which waited for: 0 -> 5; matrix products, arithmetic and copies ran while one was open for 0% -> 0% of each run, Pallas kernels for 0% -> 6%
where the time goes in v3:
time: 54.3 us; the launch traced here: 54.1 us
  waiting for transfers between devices  25.6 us (47%)
  starting transfers between devices  17.9 us (33%)
  Pallas kernels  9.85 us (18%)
  between operations  0.69 us (1%)
    ppermute x3, waiting for transfers between devices, far(): lax.ppermute(value, AXIS, [(i, i ^ d * inner) for i in range(devices)])  21.3 us
    all_to_all x1, starting transfers between devices, local(): lax.all_to_all(packed, AXIS, split_axis=0, concat_axis=0, tiled=True)  7.33 us
    ppermute x7, starting transfers between devices, local(): lax.ppermute(mixed[q], AXIS, [(i, i ^ q) for i in range(devices)])  6.31 us
    pallas_call x1, Pallas kernels, local(): pl.pallas_call(lambda *refs: late_kernel(inner, outer, *refs), out_shape=...  4.35 us
    ppermute x7, waiting for transfers between devices, local(): lax.ppermute(mixed[q], AXIS, [(i, i ^ q) for i in range(devices)])  4.33 us
    ppermute x3, starting transfers between devices, far(): lax.ppermute(value, AXIS, [(i, i ^ d * inner) for i in range(devices)])  4.29 us
    pallas_call x1, Pallas kernels, local(): pl.pallas_call(early_kernel, out_shape=(jax.ShapeDtypeStruct((1, early),...  3.39 us
    pallas_call x1, Pallas kernels, local(): pl.pallas_call(lambda *refs: pack_kernel(groups, inner, lead, *refs), out...  2.06 us
  transfers between devices with their start and end apart: 11, of which 5 were waited for; matrix products, arithmetic and copies ran while one was open for 0% of the time, Pallas kernels for 6%

profile of v3, /device:TPU:0, one launch (start us, length us, event | category | flops | bytes accessed | tf_op | source)
XLA Modules:
  0.0 54.1 jit_solution(8483158354127698567)
XLA Ops:
  0.6 2.1 %pack.1 = (bf16[32,8,1280]{2,1,0:T(8,128)(2,1)}, bf16[8,4,8,768]{3,2,1,0:T(8,128)(2,1)S(1)}, bf16[8,8,768]{2,1,0:T(8,128)(2,1)S(1)}) custom-call(s32[32]{0:T(128)} %refs_0_.1, s32[8,32]{1,0:T(8,128)} %bitcast.7, bf16[32,8,2048]{2,1,0:T(8,128)(2,1)} %bitcast.6), custom_call_target="tpu_custom_call" | custom-call | tf_op jit(solution)/shard_map/pack/pallas_call | solution.py:224
  2.7 7.3 %all-to-all-start = ((bf16[32,8,1280]{2,1,0:T(8,128)(2,1)}), bf16[32,8,1280]{2,1,0:T(8,128)(2,1)S(1)}, u32[]{:S(2)}, u32[]{:S(2)}) async-start(bf16[32,8,1280]{2,1,0:T(8,128)(2,1)} %get-tuple-element.23), calls=%async_computation | async-start | bytes 1310720 | tf_op jit(solution)/shard_map/all_to_all | solution.py:250
  10.0 2.7 %collective-permute-start = (bf16[8,8,768]{2,1,0:T(8,128)(2,1)S(1)}, bf16[8,8,768]{2,1,0:T(8,128)(2,1)S(1)}, u32[]{:S(2)}, u32[]{:S(2)}) collective-permute-start(bf16[8,8,768]{2,1,0:T(8,128)(2,1)S(1)} %get-tuple-element.30), channel_id=1, source_target_pairs={{0,16},{1,17},{2,18},{3,19},{4,20},{5,21},{6,22},{7,23},{8,24},{9,... | collective-permute-start | bytes 294920 | tf_op jit(solution)/shard_map/ppermute | solution.py:247
  12.8 19.3 %collective-permute-done.refs_1_ = bf16[8,8,768]{2,1,0:T(8,128)(2,1)S(1)} collective-permute-done((bf16[8,8,768]{2,1,0:T(8,128)(2,1)S(1)}, bf16[8,8,768]{2,1,0:T(8,128)(2,1)S(1)}, u32[]{:S(2)}, u32[]{:S(2)}) %collective-permute-start) | collective-permute-done | bytes 98336 | tf_op jit(solution)/shard_map/ppermute | solution.py:247
  32.1 0.1 collective-permute-start.1
  32.1 1.5 %collective-permute-start.2 = (bf16[4,8,768]{2,1,0:T(8,128)(2,1)S(1)}, bf16[4,8,768]{2,1,0:T(8,128)(2,1)S(1)}, u32[]{:S(2)}, u32[]{:S(2)}) collective-permute-start(bf16[4,8,768]{2,1,0:T(8,128)(2,1)S(1)} %get-tuple-element.33), channel_id=1, source_target_pairs={{0,2},{1,3},{2,0},{3,1},{4,6},{5,7},{6,4},{7,5},{8,10},{9,11},{10,... | collective-permute-start | bytes 147464 | tf_op jit(solution)/shard_map/ppermute | solution.py:261
  33.7 0.3 collective-permute-start.3
  34.0 1.5 %collective-permute-start.4 = (bf16[4,8,768]{2,1,0:T(8,128)(2,1)S(1)}, bf16[4,8,768]{2,1,0:T(8,128)(2,1)S(1)}, u32[]{:S(2)}, u32[]{:S(2)}) collective-permute-start(bf16[4,8,768]{2,1,0:T(8,128)(2,1)S(1)} %get-tuple-element.35), channel_id=1, source_target_pairs={{0,4},{1,5},{2,6},{3,7},{4,0},{5,1},{6,2},{7,3},{8,12},{9,13},{10,... | collective-permute-start | bytes 147464 | tf_op jit(solution)/shard_map/ppermute | solution.py:261
  35.5 0.2 collective-permute-start.5
  35.7 0.0 collective-permute-done.1.refs_1_
  35.7 2.4 %collective-permute-start.6 = (bf16[4,8,768]{2,1,0:T(8,128)(2,1)S(1)}, bf16[4,8,768]{2,1,0:T(8,128)(2,1)S(1)}, u32[]{:S(2)}, u32[]{:S(2)}) collective-permute-start(bf16[4,8,768]{2,1,0:T(8,128)(2,1)S(1)} %get-tuple-element.37), channel_id=1, source_target_pairs={{0,6},{1,7},{2,4},{3,5},{4,2},{5,3},{6,0},{7,1},{8,14},{9,15},{10,... | collective-permute-start | bytes 147464 | tf_op jit(solution)/shard_map/ppermute | solution.py:261
  38.1 0.0 collective-permute-done.2.refs_2_
  38.1 0.3 collective-permute-start.7
  38.4 0.0 collective-permute-done.3.refs_3_
  38.4 0.0 collective-permute-done.4.refs_4_
  38.4 0.9 %collective-permute-done.5.refs_5_ = bf16[4,8,768]{2,1,0:T(8,128)(2,1)S(1)} collective-permute-done((bf16[4,8,768]{2,1,0:T(8,128)(2,1)S(1)}, bf16[4,8,768]{2,1,0:T(8,128)(2,1)S(1)}, u32[]{:S(2)}, u32[]{:S(2)}) %collective-permute-start.5) | collective-permute-done | bytes 49184 | tf_op jit(solution)/shard_map/ppermute | solution.py:261
  39.3 1.4 %collective-permute-done.6.refs_6_ = bf16[4,8,768]{2,1,0:T(8,128)(2,1)S(1)} collective-permute-done((bf16[4,8,768]{2,1,0:T(8,128)(2,1)S(1)}, bf16[4,8,768]{2,1,0:T(8,128)(2,1)S(1)}, u32[]{:S(2)}, u32[]{:S(2)}) %collective-permute-start.6) | collective-permute-done | bytes 49184 | tf_op jit(solution)/shard_map/ppermute | solution.py:261
  40.7 2.0 %collective-permute-done.7.refs_7_ = bf16[4,8,768]{2,1,0:T(8,128)(2,1)S(1)} collective-permute-done((bf16[4,8,768]{2,1,0:T(8,128)(2,1)S(1)}, bf16[4,8,768]{2,1,0:T(8,128)(2,1)S(1)}, u32[]{:S(2)}, u32[]{:S(2)}) %collective-permute-start.7) | collective-permute-done | bytes 49184 | tf_op jit(solution)/shard_map/ppermute | solution.py:261
  42.7 0.1 collective-permute-start.8
  42.8 1.5 %collective-permute-start.9 = (bf16[8,8,768]{2,1,0:T(8,128)(2,1)S(1)}, bf16[8,8,768]{2,1,0:T(8,128)(2,1)S(1)}, u32[]{:S(2)}, u32[]{:S(2)}) collective-permute-start(bf16[8,8,768]{2,1,0:T(8,128)(2,1)S(1)} %get-tuple-element.42), channel_id=1, source_target_pairs={{0,24},{1,25},{2,26},{3,27},{4,28},{5,29},{6,30},{7,31},{8,16},{9,... | collective-permute-start | bytes 294920 | tf_op jit(solution)/shard_map/ppermute | solution.py:247
  44.3 0.0 all-to-all-done
  44.3 3.4 %early_covariance.1 = (f32[1,1280]{1,0:T(1,128)S(1)}, f32[1,2048,2048]{2,1,0:T(8,128)}, bf16[256,1280]{1,0:T(8,128)(2,1)S(1)}, bf16[1280,256]{1,0:T(8,128)(2,1)S...) custom-call(bf16[256,1280]{1,0:T(8,128)(2,1)S(1)} %bitcast.5), custom_call_target="tpu_custom_call" | custom-call | flops 838860800 | bytes 6553600 | tf_op jit(solution)/shard_map/early_covariance/pallas_call | solution.py:272
  47.7 2.1 %collective-permute-done.8.refs_6_ = bf16[8,8,768]{2,1,0:T(8,128)(2,1)S(1)} collective-permute-done((bf16[8,8,768]{2,1,0:T(8,128)(2,1)S(1)}, bf16[8,8,768]{2,1,0:T(8,128)(2,1)S(1)}, u32[]{:S(2)}, u32[]{:S(2)}) %collective-permute-start.8) | collective-permute-done | bytes 98336 | tf_op jit(solution)/shard_map/ppermute | solution.py:247
  49.8 0.0 collective-permute-done.9.refs_8_
  49.8 4.4 %late_covariance.1 = (f32[1,2048]{1,0:T(1,128)}, f32[1,2048,2048]{2,1,0:T(8,128)}) custom-call(bf16[256,1280]{1,0:T(8,128)(2,1)S(1)} %get-tuple-element.24.refs_0_, bf16[1280,256]{1,0:T(8,128)(2,1)S(1)} %get-tuple-element.25.refs_1_, bf16[256,128]{1,0:T(8,128)(2,1)S(1)} %get-tuple-element.26.refs_2_, ...), custom_call_target="tpu_custom_call", output_to_operand_aliasing={{1}: (9, {})} | custom-call | flops 1308622848 | bytes 10223616 | tf_op jit(solution)/shard_map/late_covariance/pallas_call | solution.py:295
  (2 shorter events, 0.1 us)
Async XLA Ops:
  2.7 41.6 %all-to-all-start = ((bf16[32,8,1280]{2,1,0:T(8,128)(2,1)}), bf16[32,8,1280]{2,1,0:T(8,128)(2,1)S(1)}, u32[]{:S(2)}, u32[]{:S(2)}) async-start(bf16[32,8,1280]{2,1,0:T(8,128)(2,1)} %get-tuple-element.23), calls=%async_computation | async-start | bytes 1310720 | tf_op jit(solution)/shard_map/all_to_all | solution.py:250
  10.0 22.0 %collective-permute-start = (bf16[8,8,768]{2,1,0:T(8,128)(2,1)S(1)}, bf16[8,8,768]{2,1,0:T(8,128)(2,1)S(1)}, u32[]{:S(2)}, u32[]{:S(2)}) collective-permute-start(bf16[8,8,768]{2,1,0:T(8,128)(2,1)S(1)} %get-tuple-element.30), channel_id=1, source_target_pairs={{0,16},{1,17},{2,18},{3,19},{4,20},{5,21},{6,22},{7,23},{8,24},{9,... | collective-permute-start | bytes 294920 | tf_op jit(solution)/shard_map/ppermute | solution.py:247
  32.1 3.6 %collective-permute-start.1 = (bf16[4,8,768]{2,1,0:T(8,128)(2,1)S(1)}, bf16[4,8,768]{2,1,0:T(8,128)(2,1)S(1)}, u32[]{:S(2)}, u32[]{:S(2)}) collective-permute-start(bf16[4,8,768]{2,1,0:T(8,128)(2,1)S(1)} %get-tuple-element.32), channel_id=1, source_target_pairs={{0,1},{1,0},{2,3},{3,2},{4,5},{5,4},{6,7},{7,6},{8,9},{9,8},{10,11... | collective-permute-start | bytes 147464 | tf_op jit(solution)/shard_map/ppermute | solution.py:261
  32.1 6.0 %collective-permute-start.2 = (bf16[4,8,768]{2,1,0:T(8,128)(2,1)S(1)}, bf16[4,8,768]{2,1,0:T(8,128)(2,1)S(1)}, u32[]{:S(2)}, u32[]{:S(2)}) collective-permute-start(bf16[4,8,768]{2,1,0:T(8,128)(2,1)S(1)} %get-tuple-element.33), channel_id=1, source_target_pairs={{0,2},{1,3},{2,0},{3,1},{4,6},{5,7},{6,4},{7,5},{8,10},{9,11},{10,... | collective-permute-start | bytes 147464 | tf_op jit(solution)/shard_map/ppermute | solution.py:261
  33.7 4.7 %collective-permute-start.3 = (bf16[4,8,768]{2,1,0:T(8,128)(2,1)S(1)}, bf16[4,8,768]{2,1,0:T(8,128)(2,1)S(1)}, u32[]{:S(2)}, u32[]{:S(2)}) collective-permute-start(bf16[4,8,768]{2,1,0:T(8,128)(2,1)S(1)} %get-tuple-element.34), channel_id=1, source_target_pairs={{0,3},{1,2},{2,1},{3,0},{4,7},{5,6},{6,5},{7,4},{8,11},{9,10},{10,... | collective-permute-start | bytes 147464 | tf_op jit(solution)/shard_map/ppermute | solution.py:261
  34.0 4.4 %collective-permute-start.4 = (bf16[4,8,768]{2,1,0:T(8,128)(2,1)S(1)}, bf16[4,8,768]{2,1,0:T(8,128)(2,1)S(1)}, u32[]{:S(2)}, u32[]{:S(2)}) collective-permute-start(bf16[4,8,768]{2,1,0:T(8,128)(2,1)S(1)} %get-tuple-element.35), channel_id=1, source_target_pairs={{0,4},{1,5},{2,6},{3,7},{4,0},{5,1},{6,2},{7,3},{8,12},{9,13},{10,... | collective-permute-start | bytes 147464 | tf_op jit(solution)/shard_map/ppermute | solution.py:261
  35.5 3.8 %collective-permute-start.5 = (bf16[4,8,768]{2,1,0:T(8,128)(2,1)S(1)}, bf16[4,8,768]{2,1,0:T(8,128)(2,1)S(1)}, u32[]{:S(2)}, u32[]{:S(2)}) collective-permute-start(bf16[4,8,768]{2,1,0:T(8,128)(2,1)S(1)} %get-tuple-element.36), channel_id=1, source_target_pairs={{0,5},{1,4},{2,7},{3,6},{4,1},{5,0},{6,3},{7,2},{8,13},{9,12},{10,... | collective-permute-start | bytes 147464 | tf_op jit(solution)/shard_map/ppermute | solution.py:261
  35.7 5.0 %collective-permute-start.6 = (bf16[4,8,768]{2,1,0:T(8,128)(2,1)S(1)}, bf16[4,8,768]{2,1,0:T(8,128)(2,1)S(1)}, u32[]{:S(2)}, u32[]{:S(2)}) collective-permute-start(bf16[4,8,768]{2,1,0:T(8,128)(2,1)S(1)} %get-tuple-element.37), channel_id=1, source_target_pairs={{0,6},{1,7},{2,4},{3,5},{4,2},{5,3},{6,0},{7,1},{8,14},{9,15},{10,... | collective-permute-start | bytes 147464 | tf_op jit(solution)/shard_map/ppermute | solution.py:261
  38.1 4.6 %collective-permute-start.7 = (bf16[4,8,768]{2,1,0:T(8,128)(2,1)S(1)}, bf16[4,8,768]{2,1,0:T(8,128)(2,1)S(1)}, u32[]{:S(2)}, u32[]{:S(2)}) collective-permute-start(bf16[4,8,768]{2,1,0:T(8,128)(2,1)S(1)} %get-tuple-element.38), channel_id=1, source_target_pairs={{0,7},{1,6},{2,5},{3,4},{4,3},{5,2},{6,1},{7,0},{8,15},{9,14},{10,... | collective-permute-start | bytes 147464 | tf_op jit(solution)/shard_map/ppermute | solution.py:261
  42.7 7.0 %collective-permute-start.8 = (bf16[8,8,768]{2,1,0:T(8,128)(2,1)S(1)}, bf16[8,8,768]{2,1,0:T(8,128)(2,1)S(1)}, u32[]{:S(2)}, u32[]{:S(2)}) collective-permute-start(bf16[8,8,768]{2,1,0:T(8,128)(2,1)S(1)} %get-tuple-element.40), channel_id=1, source_target_pairs={{0,8},{1,9},{2,10},{3,11},{4,12},{5,13},{6,14},{7,15},{8,0},{9,1},... | collective-permute-start | bytes 294920 | tf_op jit(solution)/shard_map/ppermute | solution.py:247
  42.8 7.0 %collective-permute-start.9 = (bf16[8,8,768]{2,1,0:T(8,128)(2,1)S(1)}, bf16[8,8,768]{2,1,0:T(8,128)(2,1)S(1)}, u32[]{:S(2)}, u32[]{:S(2)}) collective-permute-start(bf16[8,8,768]{2,1,0:T(8,128)(2,1)S(1)} %get-tuple-element.42), channel_id=1, source_target_pairs={{0,24},{1,25},{2,26},{3,27},{4,28},{5,29},{6,30},{7,31},{8,16},{9,... | collective-permute-start | bytes 294920 | tf_op jit(solution)/shard_map/ppermute | solution.py:247

commit v4 on v3

--- a/solution.py
+++ b/solution.py
@@ -24,15 +24,21 @@
     return devices // inner, inner
 
 
+def leading_flips(outer):
+    return [1 << bit for bit in reversed(range(outer.bit_length() - 1))]
+
+
 def late_width(width):
-    return width * 6 // 16 // LANES * LANES
+    return width * 7 // 16 // LANES * LANES
 
 
 def tiles(width):
     return [(at, min(TILE, width - at)) for at in range(0, width, TILE)]
 
 
-def pack_kernel(groups, inner, lead, owner_hbm, mask_hbm, blocks_hbm, early_hbm, late_ref, lead_ref, owner, mask, blocks, wide, small, big, out_sem):
+def pack_kernel(groups, inner, leads, owner_hbm, mask_hbm, blocks_hbm, early_hbm, late_ref, *refs):
+    lead_refs = refs[: len(leads)]
+    owner, mask, blocks, wide, small, big, out_sem = refs[len(leads) :]
     classes, slots, width = blocks.shape
     early = early_hbm.shape[-1]
     each = classes // groups
@@ -81,9 +87,11 @@
         for j in range(early, width, LANES):
             late_ref[q, d, :, j - early : j - early + LANES] = blocks[c, :, j : j + LANES] * weight
 
-        @pl.when(d == lead)
-        def _():
-            lead_ref[q] = late_ref[q, d]
+        for lead, lead_ref in zip(leads, lead_refs):
+
+            @pl.when(d == lead)
+            def _(lead_ref=lead_ref):
+                lead_ref[q] = late_ref[q, d]
 
         return carry
 
@@ -91,10 +99,11 @@
     pltpu.make_async_copy(blocks.at[:, :, pl.ds(0, early)], early_hbm, out_sem).wait()
 
 
-def mix_kernel(lead, late_ref, lead_ref, *outs):
-    for q, out in enumerate(outs):
+def mix_kernel(leads, late_ref, *refs):
+    came = dict(zip(leads, refs))
+    for q, out in enumerate(refs[len(leads) :]):
         for d in range(out.shape[0]):
-            out[d] = lead_ref[q] if d == lead else late_ref[q, d]
+            out[d] = came[d][q] if d in came else late_ref[q, d]
 
 
 def repack_kernel(inner, *refs):
@@ -142,13 +151,8 @@
                 out[here, part] = second[:, k : k + LANES] * scale - total * shift[:, part]
         pltpu.make_async_copy(out.at[here], cov_ref.at[0, here, pl.ds(0, width)], cov_sem).start()
 
-    def step(i, carry):
-        block(pl.multiple_of(i * TILE, TILE), TILE)
-        return carry
-
-    lax.fori_loop(0, width // TILE, step, 0)
-    if width % TILE:
-        block(width // TILE * TILE, width % TILE)
+    for at, height in tiles(width):
+        block(at, height)
     pltpu.make_async_copy(out, cov_ref.at[0, pl.ds(0, width), pl.ds(0, width)], cov_sem).wait()
 
 
@@ -216,20 +220,20 @@
     depth = devices * slots
     bf16, f32 = jnp.bfloat16, jnp.float32
     mask = jnp.swapaxes(slot_mask[0], 0, 1)
-    groups = 8
+    groups = 4
 
     inputs = [pltpu.with_memory_space_constraint(a, pltpu.HBM) for a in (owner, mask, blocks)]
 
-    lead = outer // 2
-    packed, sorted_late, leading = pl.pallas_call(
-        lambda *refs: pack_kernel(groups, inner, lead, *refs),
+    leads = leading_flips(outer)
+    packed, sorted_late, *leading = pl.pallas_call(
+        lambda *refs: pack_kernel(groups, inner, leads, *refs),
         out_shape=(
             jax.ShapeDtypeStruct((devices, slots, early), bf16),
             jax.ShapeDtypeStruct((inner, outer, slots, late), bf16),
-            jax.ShapeDtypeStruct((inner, slots, late), bf16),
-        ),
+        )
+        + (jax.ShapeDtypeStruct((inner, slots, late), bf16),) * len(leads),
         in_specs=[HBM, HBM, HBM],
-        out_specs=(HBM, VMEM, VMEM),
+        out_specs=(HBM,) + (VMEM,) * (1 + len(leads)),
         scratch_shapes=[
             pltpu.SMEM((classes,), jnp.int32),
             pltpu.VMEM((slots, classes), jnp.int32),
@@ -246,16 +250,16 @@
     def far(d, value):
         return lax.ppermute(value, AXIS, [(i, i ^ (d * inner)) for i in range(devices)])
 
-    led = far(lead, leading)
+    led = [far(d, value) for d, value in zip(leads, leading)]
     arrived = lax.all_to_all(packed, AXIS, split_axis=0, concat_axis=0, tiled=True)
     mixed = pl.pallas_call(
-        lambda *refs: mix_kernel(lead, *refs),
+        lambda *refs: mix_kernel(leads, *refs),
         out_shape=(jax.ShapeDtypeStruct((outer, slots, late), bf16),) * inner,
-        in_specs=[VMEM] * 2,
+        in_specs=[VMEM] * (1 + len(leads)),
         out_specs=(VMEM,) * inner,
         compiler_params=pltpu.CompilerParams(vmem_limit_bytes=16 * MIB),
         name="mix",
-    )(sorted_late, led)
+    )(sorted_late, *led)
     held = [mixed[0]]
     for q in range(1, inner):
         held.append(lax.ppermute(mixed[q], AXIS, [(i, i ^ q) for i in range(devices)]))
@@ -267,7 +271,7 @@
         compiler_params=pltpu.CompilerParams(vmem_limit_bytes=16 * MIB),
         name="repack",
     )(*held)
-    parts = [part if d in (0, lead) else far(d, part) for d, part in enumerate(parts)]
+    parts = [part if d in (0, *leads) else far(d, part) for d, part in enumerate(parts)]
     rows = arrived.reshape(depth, early)
     early_mean, begun, *prepared = pl.pallas_call(
         early_kernel,

time: 54.3 us -> 54.2 us (level)
  starting transfers between devices: 17.9 us -> 19.4 us
  waiting for transfers between devices: 25.6 us -> 24.3 us
    ppermute x3, waiting for transfers between devices: 21.3 us -> 19.8 us  [far(): lax.ppermute(value, AXIS, [(i, i ^ d * inner) for i in range(devices)])]
    ppermute x3, starting transfers between devices: 4.29 us -> 5.73 us  [far(): lax.ppermute(value, AXIS, [(i, i ^ d * inner) for i in range(devices)])]
  transfers between devices with their start and end apart: 11 -> 11, of which waited for: 5 -> 5; matrix products, arithmetic and copies ran while one was open for 0% -> 0% of each run, Pallas kernels for 6% -> 5%
where the time goes in v4:
time: 54.2 us; the launch traced here: 54 us
  waiting for transfers between devices  24.3 us (45%)
  starting transfers between devices  19.4 us (36%)
  Pallas kernels  9.68 us (18%)
  between operations  0.68 us (1%)
    ppermute x3, waiting for transfers between devices, far(): lax.ppermute(value, AXIS, [(i, i ^ d * inner) for i in range(devices)])  19.8 us
    all_to_all x1, starting transfers between devices, local(): lax.all_to_all(packed, AXIS, split_axis=0, concat_axis=0, tiled=True)  7.33 us
    ppermute x7, starting transfers between devices, local(): lax.ppermute(mixed[q], AXIS, [(i, i ^ q) for i in range(devices)])  6.31 us
    ppermute x3, starting transfers between devices, far(): lax.ppermute(value, AXIS, [(i, i ^ d * inner) for i in range(devices)])  5.73 us
    pallas_call x1, Pallas kernels, local(): pl.pallas_call(lambda *refs: late_kernel(inner, outer, *refs), out_shape=...  4.69 us
    ppermute x7, waiting for transfers between devices, local(): lax.ppermute(mixed[q], AXIS, [(i, i ^ q) for i in range(devices)])  4.5 us
    pallas_call x1, Pallas kernels, local(): pl.pallas_call(early_kernel, out_shape=(jax.ShapeDtypeStruct((1, early),...  2.85 us
    pallas_call x1, Pallas kernels, local(): pl.pallas_call(lambda *refs: pack_kernel(groups, inner, leads, *refs), ou...  2.08 us
  transfers between devices with their start and end apart: 11, of which 5 were waited for; matrix products, arithmetic and copies ran while one was open for 0% of the time, Pallas kernels for 5%

profile of v4, /device:TPU:0, one launch (start us, length us, event | category | flops | bytes accessed | tf_op | source)
XLA Modules:
  0.0 54.0 jit_solution(13808197307875514541)
XLA Ops:
  0.6 2.1 %pack.1 = (bf16[32,8,1152]{2,1,0:T(8,128)(2,1)}, bf16[8,4,8,896]{3,2,1,0:T(8,128)(2,1)S(1)}, bf16[8,8,896]{2,1,0:T(8,128)(2,1)S(1)}, bf16[8,8,896]{2,1,0:T(8,128)(2,1)S(1)}) custom-call(s32[32]{0:T(128)} %refs_0_.1, s32[8,32]{1,0:T(8,128)} %bitcast.7, bf16[32,8,2048]{2,1,0:T(8,128)(2,1)} %bitcast.6), custom_call_target="tpu_custom_call" | custom-call | tf_op jit(solution)/shard_map/pack/pallas_call | solution.py:228
  2.7 7.3 %all-to-all-start = ((bf16[32,8,1152]{2,1,0:T(8,128)(2,1)}), bf16[32,8,1152]{2,1,0:T(8,128)(2,1)S(1)}, u32[]{:S(2)}, u32[]{:S(2)}) async-start(bf16[32,8,1152]{2,1,0:T(8,128)(2,1)} %get-tuple-element.24), calls=%async_computation | async-start | bytes 1179648 | tf_op jit(solution)/shard_map/all_to_all | solution.py:254
  10.1 2.7 %collective-permute-start = (bf16[8,8,896]{2,1,0:T(8,128)(2,1)S(1)}, bf16[8,8,896]{2,1,0:T(8,128)(2,1)S(1)}, u32[]{:S(2)}, u32[]{:S(2)}) collective-permute-start(bf16[8,8,896]{2,1,0:T(8,128)(2,1)S(1)} %get-tuple-element.31), channel_id=1, source_target_pairs={{0,16},{1,17},{2,18},{3,19},{4,20},{5,21},{6,22},{7,23},{8,24},{9,... | collective-permute-start | bytes 344072 | tf_op jit(solution)/shard_map/ppermute | solution.py:251
  12.8 1.5 %collective-permute-start.1 = (bf16[8,8,896]{2,1,0:T(8,128)(2,1)S(1)}, bf16[8,8,896]{2,1,0:T(8,128)(2,1)S(1)}, u32[]{:S(2)}, u32[]{:S(2)}) collective-permute-start(bf16[8,8,896]{2,1,0:T(8,128)(2,1)S(1)} %get-tuple-element.32), channel_id=1, source_target_pairs={{0,8},{1,9},{2,10},{3,11},{4,12},{5,13},{6,14},{7,15},{8,0},{9,1},... | collective-permute-start | bytes 344072 | tf_op jit(solution)/shard_map/ppermute | solution.py:251
  14.3 17.0 %collective-permute-done.refs_1_ = bf16[8,8,896]{2,1,0:T(8,128)(2,1)S(1)} collective-permute-done((bf16[8,8,896]{2,1,0:T(8,128)(2,1)S(1)}, bf16[8,8,896]{2,1,0:T(8,128)(2,1)S(1)}, u32[]{:S(2)}, u32[]{:S(2)}) %collective-permute-start) | collective-permute-done | bytes 114720 | tf_op jit(solution)/shard_map/ppermute | solution.py:251
  31.3 0.0 collective-permute-done.1.refs_2_
  31.4 0.1 collective-permute-start.2
  31.5 1.5 %collective-permute-start.3 = (bf16[4,8,896]{2,1,0:T(8,128)(2,1)S(1)}, bf16[4,8,896]{2,1,0:T(8,128)(2,1)S(1)}, u32[]{:S(2)}, u32[]{:S(2)}) collective-permute-start(bf16[4,8,896]{2,1,0:T(8,128)(2,1)S(1)} %get-tuple-element.35), channel_id=1, source_target_pairs={{0,2},{1,3},{2,0},{3,1},{4,6},{5,7},{6,4},{7,5},{8,10},{9,11},{10,... | collective-permute-start | bytes 172040 | tf_op jit(solution)/shard_map/ppermute | solution.py:265
  33.0 0.3 collective-permute-start.4
  33.3 1.5 %collective-permute-start.5 = (bf16[4,8,896]{2,1,0:T(8,128)(2,1)S(1)}, bf16[4,8,896]{2,1,0:T(8,128)(2,1)S(1)}, u32[]{:S(2)}, u32[]{:S(2)}) collective-permute-start(bf16[4,8,896]{2,1,0:T(8,128)(2,1)S(1)} %get-tuple-element.37), channel_id=1, source_target_pairs={{0,4},{1,5},{2,6},{3,7},{4,0},{5,1},{6,2},{7,3},{8,12},{9,13},{10,... | collective-permute-start | bytes 172040 | tf_op jit(solution)/shard_map/ppermute | solution.py:265
  34.8 0.2 collective-permute-start.6
  35.0 0.0 collective-permute-done.2.refs_1_
  35.0 2.4 %collective-permute-start.7 = (bf16[4,8,896]{2,1,0:T(8,128)(2,1)S(1)}, bf16[4,8,896]{2,1,0:T(8,128)(2,1)S(1)}, u32[]{:S(2)}, u32[]{:S(2)}) collective-permute-start(bf16[4,8,896]{2,1,0:T(8,128)(2,1)S(1)} %get-tuple-element.39), channel_id=1, source_target_pairs={{0,6},{1,7},{2,4},{3,5},{4,2},{5,3},{6,0},{7,1},{8,14},{9,15},{10,... | collective-permute-start | bytes 172040 | tf_op jit(solution)/shard_map/ppermute | solution.py:265
  37.4 0.0 collective-permute-done.3.refs_2_
  37.4 0.3 collective-permute-start.8
  37.7 0.0 collective-permute-done.4.refs_3_
  37.7 0.0 collective-permute-done.5.refs_4_
  37.7 1.0 %collective-permute-done.6.refs_5_ = bf16[4,8,896]{2,1,0:T(8,128)(2,1)S(1)} collective-permute-done((bf16[4,8,896]{2,1,0:T(8,128)(2,1)S(1)}, bf16[4,8,896]{2,1,0:T(8,128)(2,1)S(1)}, u32[]{:S(2)}, u32[]{:S(2)}) %collective-permute-start.6) | collective-permute-done | bytes 57376 | tf_op jit(solution)/shard_map/ppermute | solution.py:265
  38.8 1.5 %collective-permute-done.7.refs_6_ = bf16[4,8,896]{2,1,0:T(8,128)(2,1)S(1)} collective-permute-done((bf16[4,8,896]{2,1,0:T(8,128)(2,1)S(1)}, bf16[4,8,896]{2,1,0:T(8,128)(2,1)S(1)}, u32[]{:S(2)}, u32[]{:S(2)}) %collective-permute-start.7) | collective-permute-done | bytes 57376 | tf_op jit(solution)/shard_map/ppermute | solution.py:265
  40.2 2.0 %collective-permute-done.8.refs_7_ = bf16[4,8,896]{2,1,0:T(8,128)(2,1)S(1)} collective-permute-done((bf16[4,8,896]{2,1,0:T(8,128)(2,1)S(1)}, bf16[4,8,896]{2,1,0:T(8,128)(2,1)S(1)}, u32[]{:S(2)}, u32[]{:S(2)}) %collective-permute-start.8) | collective-permute-done | bytes 57376 | tf_op jit(solution)/shard_map/ppermute | solution.py:265
  42.3 1.5 %collective-permute-start.9 = (bf16[8,8,896]{2,1,0:T(8,128)(2,1)S(1)}, bf16[8,8,896]{2,1,0:T(8,128)(2,1)S(1)}, u32[]{:S(2)}, u32[]{:S(2)}) collective-permute-start(bf16[8,8,896]{2,1,0:T(8,128)(2,1)S(1)} %get-tuple-element.44), channel_id=1, source_target_pairs={{0,24},{1,25},{2,26},{3,27},{4,28},{5,29},{6,30},{7,31},{8,16},{9,... | collective-permute-start | bytes 344072 | tf_op jit(solution)/shard_map/ppermute | solution.py:251
  43.7 0.0 all-to-all-done
  43.7 2.8 %early_covariance.1 = (f32[1,1152]{1,0:T(1,128)S(1)}, f32[1,2048,2048]{2,1,0:T(8,128)}, bf16[256,1152]{1,0:T(8,128)(2,1)S(1)}, bf16[1152,256]{1,0:T(8,128)(2,1)S...) custom-call(bf16[256,1152]{1,0:T(8,128)(2,1)S(1)} %bitcast.5), custom_call_target="tpu_custom_call" | custom-call | flops 679477248 | bytes 5308416 | tf_op jit(solution)/shard_map/early_covariance/pallas_call | solution.py:276
  46.6 2.7 %collective-permute-done.9.refs_8_ = bf16[8,8,896]{2,1,0:T(8,128)(2,1)S(1)} collective-permute-done((bf16[8,8,896]{2,1,0:T(8,128)(2,1)S(1)}, bf16[8,8,896]{2,1,0:T(8,128)(2,1)S(1)}, u32[]{:S(2)}, u32[]{:S(2)}) %collective-permute-start.9) | collective-permute-done | bytes 114720 | tf_op jit(solution)/shard_map/ppermute | solution.py:251
  49.3 4.7 %late_covariance.1 = (f32[1,2048]{1,0:T(1,128)}, f32[1,2048,2048]{2,1,0:T(8,128)}) custom-call(bf16[256,1152]{1,0:T(8,128)(2,1)S(1)} %get-tuple-element.25.refs_0_, bf16[1152,256]{1,0:T(8,128)(2,1)S(1)} %get-tuple-element.26.refs_1_, bf16[256,128]{1,0:T(8,128)(2,1)S(1)} %get-tuple-element.27.refs_2_, ...), custom_call_target="tpu_custom_call", output_to_operand_aliasing={{1}: (9, {})} | custom-call | flops 1468006400 | bytes 11468800 | tf_op jit(solution)/shard_map/late_covariance/pallas_call | solution.py:299
  (2 shorter events, 0.1 us)
Async XLA Ops:
  2.7 41.0 %all-to-all-start = ((bf16[32,8,1152]{2,1,0:T(8,128)(2,1)}), bf16[32,8,1152]{2,1,0:T(8,128)(2,1)S(1)}, u32[]{:S(2)}, u32[]{:S(2)}) async-start(bf16[32,8,1152]{2,1,0:T(8,128)(2,1)} %get-tuple-element.24), calls=%async_computation | async-start | bytes 1179648 | tf_op jit(solution)/shard_map/all_to_all | solution.py:254
  10.1 21.3 %collective-permute-start = (bf16[8,8,896]{2,1,0:T(8,128)(2,1)S(1)}, bf16[8,8,896]{2,1,0:T(8,128)(2,1)S(1)}, u32[]{:S(2)}, u32[]{:S(2)}) collective-permute-start(bf16[8,8,896]{2,1,0:T(8,128)(2,1)S(1)} %get-tuple-element.31), channel_id=1, source_target_pairs={{0,16},{1,17},{2,18},{3,19},{4,20},{5,21},{6,22},{7,23},{8,24},{9,... | collective-permute-start | bytes 344072 | tf_op jit(solution)/shard_map/ppermute | solution.py:251
  12.8 18.6 %collective-permute-start.1 = (bf16[8,8,896]{2,1,0:T(8,128)(2,1)S(1)}, bf16[8,8,896]{2,1,0:T(8,128)(2,1)S(1)}, u32[]{:S(2)}, u32[]{:S(2)}) collective-permute-start(bf16[8,8,896]{2,1,0:T(8,128)(2,1)S(1)} %get-tuple-element.32), channel_id=1, source_target_pairs={{0,8},{1,9},{2,10},{3,11},{4,12},{5,13},{6,14},{7,15},{8,0},{9,1},... | collective-permute-start | bytes 344072 | tf_op jit(solution)/shard_map/ppermute | solution.py:251
  31.4 3.6 %collective-permute-start.2 = (bf16[4,8,896]{2,1,0:T(8,128)(2,1)S(1)}, bf16[4,8,896]{2,1,0:T(8,128)(2,1)S(1)}, u32[]{:S(2)}, u32[]{:S(2)}) collective-permute-start(bf16[4,8,896]{2,1,0:T(8,128)(2,1)S(1)} %get-tuple-element.34), channel_id=1, source_target_pairs={{0,1},{1,0},{2,3},{3,2},{4,5},{5,4},{6,7},{7,6},{8,9},{9,8},{10,11... | collective-permute-start | bytes 172040 | tf_op jit(solution)/shard_map/ppermute | solution.py:265
  31.5 6.0 %collective-permute-start.3 = (bf16[4,8,896]{2,1,0:T(8,128)(2,1)S(1)}, bf16[4,8,896]{2,1,0:T(8,128)(2,1)S(1)}, u32[]{:S(2)}, u32[]{:S(2)}) collective-permute-start(bf16[4,8,896]{2,1,0:T(8,128)(2,1)S(1)} %get-tuple-element.35), channel_id=1, source_target_pairs={{0,2},{1,3},{2,0},{3,1},{4,6},{5,7},{6,4},{7,5},{8,10},{9,11},{10,... | collective-permute-start | bytes 172040 | tf_op jit(solution)/shard_map/ppermute | solution.py:265
  33.0 4.7 %collective-permute-start.4 = (bf16[4,8,896]{2,1,0:T(8,128)(2,1)S(1)}, bf16[4,8,896]{2,1,0:T(8,128)(2,1)S(1)}, u32[]{:S(2)}, u32[]{:S(2)}) collective-permute-start(bf16[4,8,896]{2,1,0:T(8,128)(2,1)S(1)} %get-tuple-element.36), channel_id=1, source_target_pairs={{0,3},{1,2},{2,1},{3,0},{4,7},{5,6},{6,5},{7,4},{8,11},{9,10},{10,... | collective-permute-start | bytes 172040 | tf_op jit(solution)/shard_map/ppermute | solution.py:265
  33.3 4.4 %collective-permute-start.5 = (bf16[4,8,896]{2,1,0:T(8,128)(2,1)S(1)}, bf16[4,8,896]{2,1,0:T(8,128)(2,1)S(1)}, u32[]{:S(2)}, u32[]{:S(2)}) collective-permute-start(bf16[4,8,896]{2,1,0:T(8,128)(2,1)S(1)} %get-tuple-element.37), channel_id=1, source_target_pairs={{0,4},{1,5},{2,6},{3,7},{4,0},{5,1},{6,2},{7,3},{8,12},{9,13},{10,... | collective-permute-start | bytes 172040 | tf_op jit(solution)/shard_map/ppermute | solution.py:265
  34.8 4.0 %collective-permute-start.6 = (bf16[4,8,896]{2,1,0:T(8,128)(2,1)S(1)}, bf16[4,8,896]{2,1,0:T(8,128)(2,1)S(1)}, u32[]{:S(2)}, u32[]{:S(2)}) collective-permute-start(bf16[4,8,896]{2,1,0:T(8,128)(2,1)S(1)} %get-tuple-element.38), channel_id=1, source_target_pairs={{0,5},{1,4},{2,7},{3,6},{4,1},{5,0},{6,3},{7,2},{8,13},{9,12},{10,... | collective-permute-start | bytes 172040 | tf_op jit(solution)/shard_map/ppermute | solution.py:265
  35.0 5.2 %collective-permute-start.7 = (bf16[4,8,896]{2,1,0:T(8,128)(2,1)S(1)}, bf16[4,8,896]{2,1,0:T(8,128)(2,1)S(1)}, u32[]{:S(2)}, u32[]{:S(2)}) collective-permute-start(bf16[4,8,896]{2,1,0:T(8,128)(2,1)S(1)} %get-tuple-element.39), channel_id=1, source_target_pairs={{0,6},{1,7},{2,4},{3,5},{4,2},{5,3},{6,0},{7,1},{8,14},{9,15},{10,... | collective-permute-start | bytes 172040 | tf_op jit(solution)/shard_map/ppermute | solution.py:265
  37.4 4.8 %collective-permute-start.8 = (bf16[4,8,896]{2,1,0:T(8,128)(2,1)S(1)}, bf16[4,8,896]{2,1,0:T(8,128)(2,1)S(1)}, u32[]{:S(2)}, u32[]{:S(2)}) collective-permute-start(bf16[4,8,896]{2,1,0:T(8,128)(2,1)S(1)} %get-tuple-element.40), channel_id=1, source_target_pairs={{0,7},{1,6},{2,5},{3,4},{4,3},{5,2},{6,1},{7,0},{8,15},{9,14},{10,... | collective-permute-start | bytes 172040 | tf_op jit(solution)/shard_map/ppermute | solution.py:265
  42.3 7.1 %collective-permute-start.9 = (bf16[8,8,896]{2,1,0:T(8,128)(2,1)S(1)}, bf16[8,8,896]{2,1,0:T(8,128)(2,1)S(1)}, u32[]{:S(2)}, u32[]{:S(2)}) collective-permute-start(bf16[8,8,896]{2,1,0:T(8,128)(2,1)S(1)} %get-tuple-element.44), channel_id=1, source_target_pairs={{0,24},{1,25},{2,26},{3,27},{4,28},{5,29},{6,30},{7,31},{8,16},{9,... | collective-permute-start | bytes 344072 | tf_op jit(solution)/shard_map/ppermute | solution.py:251
